TPU v7x, 32 devices: a whole 2x2x4 slice. The times are simulated.
32 devices in a mesh: branch: 2 (over core), dp: 4 (over y, x), mp: 4 (over z).
Axes of the slice: x: 2, y: 2, z: 4, core: 2. Of those that a mesh axis runs over, the one named last changes fastest.
Arguments:
- unet_hidden: bfloat16 [8, 1280, 256], P(('branch', 'dp'), 'mp'), may hold values from -6 to 6
- control_hidden: bfloat16 [2, 2, 4, 1280, 256], P('branch', None, 'dp', 'mp'), may hold values from -6 to 6
- timesteps: int32 [2, 4], P(None, 'dp'), may hold values from 0 to 999
- control_scales: int32 [2, 2, 4], P('branch', None, 'dp'), may hold values from 1 to 16
- unet_time_first: bfloat16 [320, 1280], replicated, may hold values from -0.3125 to 0.3125
- unet_time_second: bfloat16 [1280, 1280], replicated, may hold values from -0.15625 to 0.15625
- unet_proj: bfloat16 [1280, 1280], P(None, 'mp'), may hold values from -0.15625 to 0.15625
- unet_conv_first: bfloat16 [9, 1280, 1280], P(None, 'mp'), may hold values from -0.0546875 to 0.0546875
- unet_conv_second: bfloat16 [9, 1280, 1280], P(None, 'mp'), may hold values from -0.0546875 to 0.0546875
- control_time_first: bfloat16 [2, 320, 1280], P('branch'), may hold values from -0.3125 to 0.3125
- control_time_second: bfloat16 [2, 1280, 1280], P('branch'), may hold values from -0.15625 to 0.15625
- control_proj: bfloat16 [2, 1280, 1280], P('branch', None, 'mp'), may hold values from -0.15625 to 0.15625
- control_conv_first: bfloat16 [2, 9, 1280, 1280], P('branch', None, 'mp'), may hold values from -0.0546875 to 0.0546875
- control_conv_second: bfloat16 [2, 9, 1280, 1280], P('branch', None, 'mp'), may hold values from -0.0546875 to 0.0546875
- zero_conv: bfloat16 [2, 1280, 1280], P('branch', 'mp'), may hold values from -0.15625 to 0.15625
Outputs:
- skip_out: bfloat16 [8, 1280, 256], P(('branch', 'dp'), 'mp')
All inputs are finite; a program needn't handle non-finite values.
Results may differ from a plain program's by a relative error of at most 0.018.
Values may be sent and summed in bfloat16 or wider, within the bound.
A program may use at most 128 MiB of HBM per device.

v0:
```python
import functools
import math

import jax
import jax.numpy as jnp
from jax import lax
from jax.experimental import pallas as pl
from jax.experimental.pallas import tpu as pltpu
from jax.sharding import PartitionSpec as P

TDIM = 320
GROUP = 40
PIECES = 2
SIDE = 16
MESH = pl.DeviceIdType.MESH


def sinusoid(step_ids):
    half_width = TDIM // 2
    frequency = jnp.exp(-math.log(10000.0) * jnp.arange(half_width, dtype=jnp.float32) / half_width)
    angles = step_ids.astype(jnp.float32)[:, None] * frequency[None, :]
    return jnp.concatenate([jnp.cos(angles), jnp.sin(angles)], axis=1)


def norm_silu(values):
    width, pixels = values.shape
    grouped = values.reshape(width // GROUP, GROUP, pixels)
    count = 1.0 / (GROUP * pixels)
    mean = jnp.sum(jnp.sum(grouped, axis=1, keepdims=True), axis=2, keepdims=True) * count
    centered = grouped - mean
    var = jnp.sum(jnp.sum(centered * centered, axis=1, keepdims=True), axis=2, keepdims=True) * count
    normed = centered * lax.rsqrt(var + 1e-05)
    return jax.nn.silu(normed).reshape(width, pixels)


def kernel(
    ways,
    unet_hidden,
    control_hidden,
    waves,
    scale,
    hbm_time_first_c,
    hbm_time_second_c,
    hbm_proj_c,
    hbm_time_first_u,
    hbm_time_second_u,
    hbm_proj_u,
    first_c,
    second_c,
    first_u,
    second_u,
    zero,
    out,
    time_first,
    time_second,
    proj,
    w1c,
    w2c,
    w1u,
    w2u,
    wz,
    gathered,
    start,
    inner,
    flipped,
    total_c,
    total_u,
    sends,
    lands,
    swap_out,
    swap_in,
    load_sem,
    ag_send,
    ag_recv,
    rs_send,
    rs_recv,
    swap_send,
    swap_recv,
):
    branch = lax.axis_index("branch")
    dp = lax.axis_index("dp")
    me = lax.axis_index("mp")
    width, pixels = unet_hidden.shape[1], unet_hidden.shape[2]
    channels = ways * width
    last = ways - 1

    loads = [
        pltpu.make_async_copy(src, dst, load_sem.at[i])
        for i, (src, dst) in enumerate(
            (
                (hbm_time_first_c, time_first.at[0]),
                (hbm_time_second_c, time_second.at[0]),
                (hbm_proj_c, proj.at[0]),
                (hbm_time_first_u, time_first.at[1]),
                (hbm_time_second_u, time_second.at[1]),
                (hbm_proj_u, proj.at[1]),
                (first_c, w1c),
                (second_c, w2c),
                (first_u, w1u),
                (second_u, w2u),
                (zero, wz),
            )
        )
    ]
    for load in loads:
        load.start()

    barrier = pltpu.get_barrier_semaphore()

    def greet(inside, coord):
        @pl.when(inside)
        def _():
            pl.semaphore_signal(barrier, inc=1, device_id=coord, device_id_type=MESH)

    greet(me < last, (branch, dp, me + 1))
    greet(me > 0, (branch, dp, me - 1))
    pl.semaphore_signal(barrier, inc=1, device_id=(1 - branch, dp, me), device_id_type=MESH)

    def wait_barrier():
        edge = (me == 0) | (me == last)

        @pl.when(edge)
        def _():
            pl.semaphore_wait(barrier, 2)

        @pl.when(jnp.logical_not(edge))
        def _():
            pl.semaphore_wait(barrier, 3)

    def part(piece):
        return pl.ds(piece * (pixels // PIECES), pixels // PIECES)

    def ag_copy(unit, side, hop, slot, piece):
        return pltpu.make_async_remote_copy(
            src_ref=gathered.at[unit, slot, :, part(piece)],
            dst_ref=gathered.at[unit, slot, :, part(piece)],
            send_sem=ag_send.at[unit, side, hop, piece],
            recv_sem=ag_recv.at[unit, side, hop, piece],
            device_id=(branch, dp, me + 1 - 2 * side),
            device_id_type=MESH,
        )

    def ag_step(unit, hop, waits=True, sends_on=True):
        for piece, side in [(p, d) for p in range(PIECES) for d in range(2)]:
            from_slot = me - hop if side == 0 else me + hop
            here = (from_slot >= 0) & (from_slot <= last)
            onward = here & ((me < last) if side == 0 else (me > 0))

            if waits:

                @pl.when(here)
                def _():
                    ag_copy(unit, side, hop - 1, from_slot, piece).wait_recv()

            if sends_on:

                @pl.when(onward)
                def _():
                    ag_copy(unit, side, hop, from_slot, piece).start()

    def ag_drain(unit):
        for hop in range(last):
            for side in range(2):
                from_slot = me - hop if side == 0 else me + hop
                here = (from_slot >= 0) & (from_slot <= last)
                onward = here & ((me < last) if side == 0 else (me > 0))

                @pl.when(onward)
                def _():
                    for piece in range(PIECES):
                        ag_copy(unit, side, hop, from_slot, piece).wait_send()

    def rs_copy(unit, side, dest, piece):
        return pltpu.make_async_remote_copy(
            src_ref=sends.at[unit, dest, :, part(piece)],
            dst_ref=lands.at[unit, side, dest, :, part(piece)],
            send_sem=rs_send.at[unit, dest, piece],
            recv_sem=rs_recv.at[unit, side, dest, piece],
            device_id=(branch, dp, me + 1 - 2 * side),
            device_id_type=MESH,
        )

    def rs_start(unit):
        @pl.when(me == 0)
        def _():
            for dest in range(last, 0, -1):
                for piece in range(PIECES):
                    rs_copy(unit, 0, dest, piece).start()

        @pl.when(me == last)
        def _():
            for dest in range(last):
                for piece in range(PIECES):
                    rs_copy(unit, 1, dest, piece).start()

    def rs_slot(unit, slot):
        for piece, side in [(p, d) for p in range(PIECES) for d in range(2)]:
            place = me if side == 0 else last - me
            dest = last - slot + place if side == 0 else slot - place

            @pl.when((place >= 1) & (place <= slot))
            def _():
                rs_copy(unit, side, dest, piece).wait_recv()
                added = sends[unit, dest, :, part(piece)].astype(jnp.float32) + lands[
                    unit, side, dest, :, part(piece)
                ].astype(jnp.float32)
                sends[unit, dest, :, part(piece)] = added.astype(jnp.bfloat16)
                rs_copy(unit, side, dest, piece).start()

    def rs_drain(unit):
        for dest in range(ways):

            @pl.when(dest > me)
            def _():
                for piece in range(PIECES):
                    rs_copy(unit, 0, dest, piece).wait_send()

            @pl.when(dest < me)
            def _():
                for piece in range(PIECES):
                    rs_copy(unit, 1, dest, piece).wait_send()

    def own_hidden(unit):
        if unit == 2:
            return unet_hidden[0]
        half = 1 - branch if unit == 0 else branch
        return control_hidden[0, half, 0]

    def prepare(unit):
        gathered[unit, me] = norm_silu(own_hidden(unit).astype(jnp.float32)).astype(jnp.bfloat16)

    def embed(block):
        for load in loads[3 * block : 3 * block + 3]:
            load.wait()
        act = waves[...]
        for weight in (time_first, time_second):
            act = jax.nn.silu(
                jnp.dot(act, weight[block], preferred_element_type=jnp.float32)
            ).astype(jnp.bfloat16)
        start[block] = lax.dot_general(
            proj[block], act, (((1,), (1,)), ((), ())), preferred_element_type=jnp.float32
        )

    def keep_of(tap, shape, axis):
        dy = tap // 3 - 1
        dx = lax.rem(tap, 3) - 1
        spot = lax.broadcasted_iota(jnp.int32, shape, axis)
        row = spot // SIDE + dy
        col = lax.rem(spot, SIDE) + dx
        keep = (row >= 0) & (row < SIDE) & (col >= 0) & (col < SIDE)
        return keep, lax.rem(2 * pixels - (SIDE * dy + dx), pixels)

    def block(unit, first_weight, second_weight, total, first_load, second_load, hooks):
        ag_step(unit, last, sends_on=False)
        if first_load is not None:
            first_load.wait()
        other = branch == 1 if unit == 0 else branch == 0
        columns = start[unit // 2]
        inner[...] = jnp.broadcast_to(
            jnp.where(other, columns[:, :1], columns[:, 1:2]), (width, pixels)
        )

        def run(step):
            for place, hook in hooks:
                pl.when(step == place)(hook)

        def first_tap(tap, carry):
            run(tap)
            term = jnp.dot(
                first_weight[tap],
                gathered[unit].reshape(channels, pixels),
                preferred_element_type=jnp.float32,
            )
            keep, shift = keep_of(tap, (1, pixels), 1)
            inner[...] += jnp.where(keep, pltpu.roll(term, shift, 1), 0.0)
            return carry

        lax.fori_loop(0, 9, first_tap, 0)
        flipped[...] = norm_silu(inner[...]).T
        if second_load is not None:
            second_load.wait()
        total[...] = jnp.zeros_like(total)

        def second_line(line, carry):
            operands = []
            for side in range(3):
                tap = 3 * line + side
                run(tap + 9)
                keep, shift = keep_of(tap, (pixels, 1), 0)
                moved = pltpu.roll(flipped[...], shift, 0)
                operands.append(jnp.where(keep, moved, 0.0).astype(jnp.bfloat16))
            total[...] += jnp.dot(
                jnp.concatenate(operands, axis=1),
                second_weight[pl.ds(3 * line, 3)].reshape(3 * width, channels),
                preferred_element_type=jnp.float32,
            )
            return carry

        lax.fori_loop(0, 3, second_line, 0)

    def scatter(unit, total):
        sends[unit] = total[...].T.astype(jnp.bfloat16).reshape(ways, width, pixels)
        rs_start(unit)

    def collect(unit):
        inner[...] = own_hidden(unit).astype(jnp.float32) + sends[unit, me].astype(jnp.float32)
        for side, inside in ((0, me > 0), (1, me < last)):

            @pl.when(inside)
            def _():
                for piece in range(PIECES):
                    rs_copy(unit, side, me, piece).wait_recv()
                inner[...] += lands[unit, side, me].astype(jnp.float32)

        return inner[...]

    def residual(unit):
        half = 1 - branch if unit == 0 else branch
        copy_out = collect(unit).T.astype(jnp.bfloat16)
        term = jnp.dot(copy_out, wz[...], preferred_element_type=jnp.float32)
        return term * (scale[half, 0].astype(jnp.float32) * 0.125)

    def spread(first, span, count):
        return [first + i * span // max(count, 1) for i in range(count)]

    prepare(0)
    wait_barrier()
    ag_step(0, 0, waits=False)
    prepare(1)
    prepare(2)
    relays = range(1, last)
    for hop in relays:
        ag_step(0, hop)
        if hop == 1:
            embed(0)
    ag_step(1, 0, waits=False)
    embed(1)

    def relay_hook(unit, hop):
        def hook():
            ag_step(unit, hop)
            if unit == 1 and hop == last - 1:
                ag_step(2, 0, waits=False)

        return hook

    def slot_hook(unit, slot):
        return lambda: rs_slot(unit, slot)

    block(
        0, w1c, w2c, total_c, loads[6], loads[7],
        [(p, relay_hook(1, h)) for p, h in zip(spread(4, 12, len(relays)), relays)],
    )
    scatter(0, total_c)
    block(
        1, w1c, w2c, total_c, None, None,
        [(p, relay_hook(2, h)) for p, h in zip(spread(1, 12, len(relays)), relays)]
        + [(p, slot_hook(0, k)) for p, k in zip(spread(8, 10, len(relays)), relays)],
    )
    scatter(1, total_c)
    loads[10].wait()
    swap_out[...] = residual(0).astype(jnp.bfloat16)
    swap = pltpu.make_async_remote_copy(
        src_ref=swap_out,
        dst_ref=swap_in,
        send_sem=swap_send,
        recv_sem=swap_recv,
        device_id=(1 - branch, dp, me),
        device_id_type=MESH,
    )
    swap.start()
    block(
        2, w1u, w2u, total_u, loads[8], loads[9],
        [(p, slot_hook(1, k)) for p, k in zip(spread(6, 12, len(relays)), relays)],
    )
    total_u[...] += residual(1)
    swap.wait_recv()
    total_u[...] += swap_in[...].astype(jnp.float32)
    scatter(2, total_u)
    for slot in relays:
        rs_slot(2, slot)
    out[0] = collect(2).astype(jnp.bfloat16)
    swap.wait_send()
    for unit in range(3):
        ag_drain(unit)
        rs_drain(unit)


def shards(
    unet_hidden,
    control_hidden,
    timesteps,
    control_scales,
    unet_time_first,
    unet_time_second,
    unet_proj,
    unet_conv_first,
    unet_conv_second,
    control_time_first,
    control_time_second,
    control_proj,
    control_conv_first,
    control_conv_second,
    zero_conv,
):
    ways = lax.axis_size("mp")
    width, pixels = unet_hidden.shape[1], unet_hidden.shape[2]
    channels = ways * width
    halves = timesteps.shape[0]
    waves = sinusoid(timesteps.reshape(halves)).astype(jnp.bfloat16)
    waves = jnp.pad(waves, ((0, 16 - halves), (0, 0)))
    scale = control_scales[0]
    vmem = pl.BlockSpec(memory_space=pltpu.VMEM)
    hbm = pl.BlockSpec(memory_space=pl.ANY)
    taps = unet_conv_first.shape[0]
    bf16, f32 = jnp.bfloat16, jnp.float32
    conv_shape = (taps, width, channels)
    return pl.pallas_call(
        functools.partial(kernel, ways),
        out_shape=jax.ShapeDtypeStruct((1, width, pixels), bf16),
        in_specs=[vmem] * 3 + [pl.BlockSpec(memory_space=pltpu.SMEM)] + [hbm] * 11,
        out_specs=vmem,
        scratch_shapes=[
            pltpu.VMEM((2,) + unet_time_first.shape, bf16),
            pltpu.VMEM((2,) + unet_time_second.shape, bf16),
            pltpu.VMEM((2,) + unet_proj.shape[::-1], bf16),
            pltpu.VMEM(conv_shape, bf16),
            pltpu.VMEM(conv_shape, bf16),
            pltpu.VMEM(conv_shape, bf16),
            pltpu.VMEM(conv_shape, bf16),
            pltpu.VMEM((width, channels), bf16),
            pltpu.VMEM((3, ways, width, pixels), bf16),
            pltpu.VMEM((2, width, 16), f32),
            pltpu.VMEM((width, pixels), f32),
            pltpu.VMEM((pixels, width), f32),
            pltpu.VMEM((pixels, channels), f32),
            pltpu.VMEM((pixels, channels), f32),
            pltpu.VMEM((3, ways, width, pixels), bf16),
            pltpu.VMEM((3, 2, ways, width, pixels), bf16),
            pltpu.VMEM((pixels, channels), bf16),
            pltpu.VMEM((pixels, channels), bf16),
            pltpu.SemaphoreType.DMA((11,)),
            pltpu.SemaphoreType.DMA((3, 2, ways - 1, PIECES)),
            pltpu.SemaphoreType.DMA((3, 2, ways - 1, PIECES)),
            pltpu.SemaphoreType.DMA((3, ways, PIECES)),
            pltpu.SemaphoreType.DMA((3, 2, ways, PIECES)),
            pltpu.SemaphoreType.DMA,
            pltpu.SemaphoreType.DMA,
        ],
        compiler_params=pltpu.CompilerParams(
            collective_id=0, has_side_effects=True, vmem_limit_bytes=62 * 1024 * 1024
        ),
    )(
        unet_hidden,
        control_hidden,
        waves,
        scale,
        control_time_first[0],
        control_time_second[0],
        control_proj[0].T,
        unet_time_first,
        unet_time_second,
        unet_proj.T,
        control_conv_first[0],
        control_conv_second[0],
        unet_conv_first,
        unet_conv_second,
        zero_conv[0],
    )


def solution(mesh):
    in_specs = (
        P(("branch", "dp"), "mp", None),
        P("branch", None, "dp", "mp", None),
        P(None, "dp"),
        P("branch", None, "dp"),
        P(),
        P(),
        P(None, "mp"),
        P(None, "mp", None),
        P(None, "mp", None),
        P("branch", None, None),
        P("branch", None, None),
        P("branch", None, "mp"),
        P("branch", None, "mp", None),
        P("branch", None, "mp", None),
        P("branch", "mp", None),
    )
    out_specs = P(("branch", "dp"), "mp", None)
    return jax.shard_map(shards, mesh=mesh, in_specs=in_specs, out_specs=out_specs, check_vma=False)
```

profile of v0, /device:TPU:0, one launch (start us, length us, event | category | flops | bytes accessed | tf_op | source)
XLA Modules:
  0.0 74.7 jit_solution(12606257228831687075)
XLA Ops:
  0.0 0.7 convert_bitcast_fusion
  0.7 1.3 %copy.16.scale = s32[2,1]{1,0:T(2,128)} copy(s32[2,1]{0,1:T(1,128)} %bitcast.19) | data formatting | bytes 16 | tf_op jit(solution)/shard_map/squeeze | solution.py:412
  1.9 0.1 fusion.3
  2.1 0.7 fusion.2.waves
  2.8 70.3 %shard_map.145 = bf16[1,320,256]{2,1,0:T(8,128)(2,1)} custom-call(bf16[1,320,256]{2,1,0:T(8,128)(2,1)} %unet_hidden.1, bf16[1,2,1,320,256]{4,3,2,1,0:T(8,128)(2,1)} %control_hidden.1, bf16[16,320]{1,0:T(8,128)(2,1)} %fusion.2.waves, s32[2,1]{1,0:T(2,128)} %copy.16.scale, bf16[320,1280]{1,0:T(8,128)(2,1)} %bitcast.15, bf16[1280,1280]{1,0:T(8,128)(2,1)} %bitcast.14, ...), custom_call_target="tpu_custom_call" | custom-call | tf_op jit(solution)/shard_map/pallas_call | solution.py:418
  73.1 1.6 %copy.18 = bf16[1,320,256]{2,1,0:T(8,128)(2,1)} copy(bf16[1,320,256]{2,1,0:T(8,128)(2,1)} %shard_map.145) | data formatting | bytes 327680
  (1 shorter events, 0.0 us)
where the time goes:
time: 74.8 us; the launch traced here: 74.7 us
  Pallas kernels  70.3 us (94%)
  local copies, waits for them, and re-layouts  2.87 us (4%)
  other arithmetic  1.47 us (2%)
    pallas_call x1, Pallas kernels, shards(): pl.pallas_call(functools.partial(kernel, ways), out_shape=jax.ShapeDtypeS...  70.3 us
    unnamed x1, local copies, waits for them, and re-layouts  1.59 us

commit v1 on v0

v1 whole, which is shorter than its diff:
```python
import functools
import math

import jax
import jax.numpy as jnp
from jax import lax
from jax.experimental import pallas as pl
from jax.experimental.pallas import tpu as pltpu
from jax.sharding import PartitionSpec as P

TDIM = 320
GROUP = 40
PIECES = 2
SIDE = 16
MESH = pl.DeviceIdType.MESH


def sinusoid(steps, rows):
    half_width = TDIM // 2
    row = lax.broadcasted_iota(jnp.int32, (rows, TDIM), 0)
    spot = lax.broadcasted_iota(jnp.int32, (rows, TDIM), 1)
    place = jnp.where(spot < half_width, spot, spot - half_width).astype(jnp.float32)
    frequency = jnp.exp(-math.log(10000.0) * place / half_width)
    step = jnp.zeros((rows, TDIM), jnp.float32)
    for i, value in enumerate(steps):
        step = jnp.where(row == i, value.astype(jnp.float32), step)
    angles = step * frequency
    return jnp.where(spot < half_width, jnp.cos(angles), jnp.sin(angles))


def norm_silu(values):
    width, pixels = values.shape
    grouped = values.reshape(width // GROUP, GROUP, pixels)
    count = 1.0 / (GROUP * pixels)
    mean = jnp.sum(jnp.sum(grouped, axis=1, keepdims=True), axis=2, keepdims=True) * count
    centered = grouped - mean
    var = jnp.sum(jnp.sum(centered * centered, axis=1, keepdims=True), axis=2, keepdims=True) * count
    normed = centered * lax.rsqrt(var + 1e-05)
    return jax.nn.silu(normed).reshape(width, pixels)


def kernel(
    ways,
    unet_hidden,
    control_hidden,
    steps,
    scale,
    hbm_time_first_c,
    hbm_time_second_c,
    hbm_proj_c,
    hbm_time_first_u,
    hbm_time_second_u,
    hbm_proj_u,
    first_c,
    second_c,
    first_u,
    second_u,
    zero,
    out,
    time_first,
    time_second,
    proj,
    w1c,
    w2c,
    w1u,
    w2u,
    wz,
    gathered,
    above,
    below,
    taps,
    start,
    inner,
    sends,
    lands,
    scaled,
    swap_out,
    swap_in,
    load_sem,
    ag_send,
    ag_recv,
    rs_send,
    rs_recv,
    swap_send,
    swap_recv,
):
    branch = lax.axis_index("branch")
    dp = lax.axis_index("dp")
    me = lax.axis_index("mp")
    width, pixels = unet_hidden.shape[1], unet_hidden.shape[2]
    channels = ways * width
    last = ways - 1
    half = pixels // PIECES
    scope = jax.named_scope

    loads = [
        pltpu.make_async_copy(src, dst, load_sem.at[i])
        for i, (src, dst) in enumerate(
            (
                (hbm_time_first_c, time_first.at[0]),
                (hbm_time_second_c, time_second.at[0]),
                (hbm_proj_c, proj.at[0]),
                (hbm_time_first_u, time_first.at[1]),
                (hbm_time_second_u, time_second.at[1]),
                (hbm_proj_u, proj.at[1]),
                (first_c, w1c),
                (second_c, w2c),
                (first_u, w1u),
                (second_u, w2u),
                (zero, wz),
            )
        )
    ]
    for i in (0, 1, 2, 6):
        loads[i].start()

    barrier = pltpu.get_barrier_semaphore()

    def greet(inside, coord):
        @pl.when(inside)
        def _():
            pl.semaphore_signal(barrier, inc=1, device_id=coord, device_id_type=MESH)

    greet(me < last, (branch, dp, me + 1))
    greet(me > 0, (branch, dp, me - 1))
    pl.semaphore_signal(barrier, inc=1, device_id=(1 - branch, dp, me), device_id_type=MESH)

    def wait_barrier():
        edge = (me == 0) | (me == last)

        @pl.when(edge)
        def _():
            pl.semaphore_wait(barrier, 2)

        @pl.when(jnp.logical_not(edge))
        def _():
            pl.semaphore_wait(barrier, 3)

    def part(piece):
        return pl.ds(piece * half, half)

    def rows_of(slot):
        return pl.ds(pl.multiple_of(slot * width, width), width)

    def ag_copy(unit, side, hop, slot, piece):
        return pltpu.make_async_remote_copy(
            src_ref=gathered.at[unit, rows_of(slot), part(piece)],
            dst_ref=gathered.at[unit, rows_of(slot), part(piece)],
            send_sem=ag_send.at[unit, side, hop, piece],
            recv_sem=ag_recv.at[unit, side, hop, piece],
            device_id=(branch, dp, me + 1 - 2 * side),
            device_id_type=MESH,
        )

    middle = ways // 2

    def forward(unit, hop, sides):
        for piece in range(PIECES):
            for side in range(2):
                from_slot = me - hop if side == 0 else me + hop
                here = (from_slot >= 0) & (from_slot <= last)
                onward = here & ((me < last) if side == 0 else (me > 0)) & sides[side]

                @pl.when(onward)
                def _():
                    if hop > 0:
                        ag_copy(unit, side, hop - 1, from_slot, piece).wait_recv()
                    ag_copy(unit, side, hop, from_slot, piece).start()

    low, high = me < middle, me >= middle
    edge = (me == 0) | (me == last)
    inner_low, inner_high = low & jnp.logical_not(edge), high & jnp.logical_not(edge)
    both, inward, outward = (True, True), (low, high), (high, low)

    def ag_begin(unit, sides=both):
        forward(unit, 0, sides)

    def ag_inward(unit):
        for hop in range(1, last):
            forward(unit, hop, inward)

    def ag_outward(unit, hop):
        forward(unit, hop, outward)

    def ag_arrive(unit):
        for hop in range(1, ways):
            for side in range(2):
                from_slot = me - hop if side == 0 else me + hop
                here = (from_slot >= 0) & (from_slot <= last)
                if hop < last:
                    here = here & ((me == last) if side == 0 else (me == 0))

                @pl.when(here)
                def _():
                    for piece in range(PIECES):
                        ag_copy(unit, side, hop - 1, from_slot, piece).wait_recv()

    def ag_drain(unit):
        for hop in range(last):
            for side in range(2):
                from_slot = me - hop if side == 0 else me + hop
                here = (from_slot >= 0) & (from_slot <= last)
                onward = here & ((me < last) if side == 0 else (me > 0))

                @pl.when(onward)
                def _():
                    for piece in range(PIECES):
                        ag_copy(unit, side, hop, from_slot, piece).wait_send()

    def rs_copy(unit, side, dest, piece):
        return pltpu.make_async_remote_copy(
            src_ref=sends.at[unit, rows_of(dest), part(piece)],
            dst_ref=lands.at[unit, side, dest, :, part(piece)],
            send_sem=rs_send.at[unit, dest, piece],
            recv_sem=rs_recv.at[unit, side, dest, piece],
            device_id=(branch, dp, me + 1 - 2 * side),
            device_id_type=MESH,
        )

    def rs_start(unit):
        @pl.when(me == 0)
        def _():
            for dest in range(last, 0, -1):
                for piece in range(PIECES):
                    rs_copy(unit, 0, dest, piece).start()

        @pl.when(me == last)
        def _():
            for dest in range(last):
                for piece in range(PIECES):
                    rs_copy(unit, 1, dest, piece).start()

    def rs_slot(unit, slot):
        for piece, side in [(p, d) for p in range(PIECES) for d in range(2)]:
            place = me if side == 0 else last - me
            dest = last - slot + place if side == 0 else slot - place

            @pl.when((place >= 1) & (place <= slot))
            def _():
                rs_copy(unit, side, dest, piece).wait_recv()
                added = sends[unit, rows_of(dest), part(piece)].astype(jnp.float32) + lands[
                    unit, side, dest, :, part(piece)
                ].astype(jnp.float32)
                sends[unit, rows_of(dest), part(piece)] = added.astype(jnp.bfloat16)
                rs_copy(unit, side, dest, piece).start()

    def rs_drain(unit):
        for dest in range(ways):

            @pl.when(dest > me)
            def _():
                for piece in range(PIECES):
                    rs_copy(unit, 0, dest, piece).wait_send()

            @pl.when(dest < me)
            def _():
                for piece in range(PIECES):
                    rs_copy(unit, 1, dest, piece).wait_send()

    def own_hidden(unit):
        if unit == 2:
            return unet_hidden[0]
        image = 1 - branch if unit == 0 else branch
        return control_hidden[0, image, 0]

    def prepare(unit):
        gathered[unit, rows_of(me), :] = norm_silu(own_hidden(unit).astype(jnp.float32)).astype(
            jnp.bfloat16
        )

    def embed(block, waves):
        for load in loads[3 * block : 3 * block + 3]:
            load.wait()
        act = waves
        for weight in (time_first, time_second):
            act = jax.nn.silu(
                jnp.dot(act, weight[block], preferred_element_type=jnp.float32)
            ).astype(jnp.bfloat16)
        start[block] = lax.dot_general(
            proj[block], act, (((1,), (1,)), ((), ())), preferred_element_type=jnp.float32
        )

    def column_kept(shape, axis, dx):
        spot = lax.rem(lax.broadcasted_iota(jnp.int32, shape, axis), SIDE) + dx
        return (spot >= 0) & (spot < SIDE)

    def shift_rows(unit):
        spot = lax.broadcasted_iota(jnp.int32, (1, pixels), 1)
        whole = gathered[unit].astype(jnp.float32)
        down = pltpu.roll(whole, SIDE, 1)
        above[...] = jnp.where(spot >= SIDE, down, 0.0).astype(jnp.bfloat16)
        up = pltpu.roll(whole, pixels - SIDE, 1)
        below[...] = jnp.where(spot < pixels - SIDE, up, 0.0).astype(jnp.bfloat16)

    def first_conv(unit, weight, hook):
        shift_rows(unit)
        other = branch == 1 if unit == 0 else branch == 0
        columns = start[unit // 2]
        bias = jnp.where(other, columns[:, :1], columns[:, 1:2])

        def side_term(dx):
            term = None
            for line, source in enumerate((above[...], gathered[unit], below[...])):
                product = jnp.dot(
                    weight[3 * line + dx + 1], source, preferred_element_type=jnp.float32
                )
                term = product if term is None else term + product
            return term

        inner[...] = side_term(0) + bias
        hook(0)
        for dx in (-1, 1):
            moved = pltpu.roll(side_term(dx), (pixels - dx) % pixels, 1)
            inner[...] += jnp.where(column_kept((1, pixels), 1, dx), moved, 0.0)
            hook(dx)

    def fill_taps():
        flipped = norm_silu(inner[...]).T
        operands = []
        for dx in (-1, 0, 1):
            moved = flipped if dx == 0 else pltpu.roll(flipped, (pixels - dx) % pixels, 0)
            operands.append(jnp.where(column_kept((pixels, 1), 0, dx), moved, 0.0))
        taps[SIDE : SIDE + pixels, :] = jnp.concatenate(operands, axis=1).astype(jnp.bfloat16)

    def second_conv(unit, weight, hook):
        tile = channels // 5
        for chunk in range(5):
            at = pl.ds(chunk * tile, tile)
            total = None
            for line in range(3):
                product = jnp.dot(
                    taps[SIDE * line : SIDE * line + pixels, :],
                    weight[3 * line : 3 * line + 3, :, chunk * tile : (chunk + 1) * tile].reshape(
                        3 * width, tile
                    ),
                    preferred_element_type=jnp.float32,
                )
                total = product if total is None else total + product
            if unit == 2:
                total = total + jnp.dot(
                    scaled[...],
                    wz[:, chunk * tile : (chunk + 1) * tile],
                    preferred_element_type=jnp.float32,
                )
                total = total + swap_in[:, chunk * tile : (chunk + 1) * tile].astype(jnp.float32)
            sends[unit, at, :] = total.T.astype(jnp.bfloat16)
            hook(chunk)

    def collect(unit):
        result = own_hidden(unit).astype(jnp.float32) + sends[unit, rows_of(me), :].astype(
            jnp.float32
        )
        inner[...] = result
        for side, inside in ((0, me > 0), (1, me < last)):

            @pl.when(inside)
            def _():
                for piece in range(PIECES):
                    rs_copy(unit, side, me, piece).wait_recv()
                inner[...] += lands[unit, side, me].astype(jnp.float32)

        return inner[...]

    def scale_copy(unit):
        image = 1 - branch if unit == 0 else branch
        factor = scale[0, image].astype(jnp.float32) * 0.125
        scaled[...] = (collect(unit) * factor).T.astype(jnp.bfloat16)

    def quiet(place):
        pass

    taps[0:SIDE, :] = jnp.zeros((SIDE, 3 * width), jnp.bfloat16)
    taps[SIDE + pixels :, :] = jnp.zeros((SIDE, 3 * width), jnp.bfloat16)

    hops = range(1, last)
    with scope("prep"):
        for unit in range(3):
            prepare(unit)
        waves = sinusoid([steps[0, i] for i in range(steps.shape[1])], 16).astype(jnp.bfloat16)
    with scope("barrier"):
        wait_barrier()
    with scope("ag0"):
        ag_begin(0)
        for unit in (1, 2):
            ag_begin(unit, (me == 0, me == last))
    with scope("embed0"):
        embed(0, waves)
        for i in (7, 3, 4, 5):
            loads[i].start()
    for hop in hops:
        with scope(f"ag0_hop{hop}"):
            forward(0, hop, both)
            if hop == 1:
                ag_begin(1, (inner_low, inner_high))
    with scope("ag1"):
        ag_begin(1, outward)
        ag_inward(1)
    with scope("ag0_wait"):
        ag_arrive(0)
    with scope("w1c_wait"):
        loads[6].wait()
    with scope("conv1_0"):
        first_conv(0, w1c, quiet)
    with scope("ag2_in"):
        ag_begin(2, (inner_low, inner_high))
        ag_inward(2)
    with scope("ag1_out1"):
        ag_outward(1, 1)
    with scope("w2c_wait"):
        loads[7].wait()
    with scope("fill0"):
        fill_taps()
    with scope("conv2_0"):
        second_conv(0, w2c, quiet)
    for hop in hops[1:]:
        with scope(f"ag1_out{hop}"):
            ag_outward(1, hop)
    with scope("ag2"):
        ag_begin(2, outward)
    with scope("rs0"):
        rs_start(0)
        for i in (8, 9, 10):
            loads[i].start()
    with scope("embed1"):
        embed(1, waves)
    with scope("rs0_slot1"):
        rs_slot(0, 1)
    with scope("ag1_wait"):
        ag_arrive(1)
    with scope("conv1_1"):
        first_conv(1, w1c, quiet)
    with scope("ag2_out1"):
        ag_outward(2, 1)
    with scope("rs0_slot2"):
        for slot in hops[1:]:
            rs_slot(0, slot)
    with scope("fill1"):
        fill_taps()
    with scope("conv2_1"):
        second_conv(1, w2c, quiet)
    for hop in hops[1:]:
        with scope(f"ag2_out{hop}"):
            ag_outward(2, hop)
    with scope("rs1"):
        rs_start(1)
    with scope("res0"):
        loads[10].wait()
        scale_copy(0)
        swap_out[...] = jnp.dot(scaled[...], wz[...], preferred_element_type=jnp.float32).astype(
            jnp.bfloat16
        )
    swap = pltpu.make_async_remote_copy(
        src_ref=swap_out,
        dst_ref=swap_in,
        send_sem=swap_send,
        recv_sem=swap_recv,
        device_id=(1 - branch, dp, me),
        device_id_type=MESH,
    )
    swap.start()
    with scope("rs1_slot1"):
        rs_slot(1, 1)
    with scope("ag2_wait"):
        ag_arrive(2)
        loads[8].wait()
        loads[9].wait()
    with scope("conv1_2"):
        first_conv(2, w1u, quiet)
    with scope("rs1_slot2"):
        for slot in hops[1:]:
            rs_slot(1, slot)
    with scope("fill2"):
        fill_taps()
    with scope("res1"):
        scale_copy(1)
    with scope("swap_wait"):
        swap.wait_recv()
    with scope("conv2_2"):
        second_conv(2, w2u, quiet)
    with scope("rs2"):
        rs_start(2)
    for slot in hops:
        with scope(f"rs2_slot{slot}"):
            rs_slot(2, slot)
    with scope("collect2"):
        out[0] = collect(2).astype(jnp.bfloat16)
    swap.wait_send()
    for unit in range(3):
        ag_drain(unit)
        rs_drain(unit)

def shards(
    unet_hidden,
    control_hidden,
    timesteps,
    control_scales,
    unet_time_first,
    unet_time_second,
    unet_proj,
    unet_conv_first,
    unet_conv_second,
    control_time_first,
    control_time_second,
    control_proj,
    control_conv_first,
    control_conv_second,
    zero_conv,
):
    ways = lax.axis_size("mp")
    width, pixels = unet_hidden.shape[1], unet_hidden.shape[2]
    channels = ways * width
    halves = timesteps.shape[0]
    steps = timesteps.reshape(1, halves)
    scale = control_scales.reshape(1, halves)
    vmem = pl.BlockSpec(memory_space=pltpu.VMEM)
    smem = pl.BlockSpec(memory_space=pltpu.SMEM)
    hbm = pl.BlockSpec(memory_space=pl.ANY)
    taps = unet_conv_first.shape[0]
    bf16, f32 = jnp.bfloat16, jnp.float32
    conv_shape = (taps, width, channels)
    return pl.pallas_call(
        functools.partial(kernel, ways),
        out_shape=jax.ShapeDtypeStruct((1, width, pixels), bf16),
        in_specs=[vmem] * 2 + [smem] * 2 + [hbm] * 11,
        out_specs=vmem,
        scratch_shapes=[
            pltpu.VMEM((2,) + unet_time_first.shape, bf16),
            pltpu.VMEM((2,) + unet_time_second.shape, bf16),
            pltpu.VMEM((2,) + unet_proj.shape[::-1], bf16),
            pltpu.VMEM(conv_shape, bf16),
            pltpu.VMEM(conv_shape, bf16),
            pltpu.VMEM(conv_shape, bf16),
            pltpu.VMEM(conv_shape, bf16),
            pltpu.VMEM((width, channels), bf16),
            pltpu.VMEM((3, channels, pixels), bf16),
            pltpu.VMEM((channels, pixels), bf16),
            pltpu.VMEM((channels, pixels), bf16),
            pltpu.VMEM((pixels + 2 * SIDE, 3 * width), bf16),
            pltpu.VMEM((2, width, 16), f32),
            pltpu.VMEM((width, pixels), f32),
            pltpu.VMEM((3, channels, pixels), bf16),
            pltpu.VMEM((3, 2, ways, width, pixels), bf16),
            pltpu.VMEM((pixels, width), bf16),
            pltpu.VMEM((pixels, channels), bf16),
            pltpu.VMEM((pixels, channels), bf16),
            pltpu.SemaphoreType.DMA((11,)),
            pltpu.SemaphoreType.DMA((3, 2, ways - 1, PIECES)),
            pltpu.SemaphoreType.DMA((3, 2, ways - 1, PIECES)),
            pltpu.SemaphoreType.DMA((3, ways, PIECES)),
            pltpu.SemaphoreType.DMA((3, 2, ways, PIECES)),
            pltpu.SemaphoreType.DMA,
            pltpu.SemaphoreType.DMA,
        ],
        compiler_params=pltpu.CompilerParams(
            collective_id=0, has_side_effects=True, vmem_limit_bytes=62 * 1024 * 1024
        ),
    )(
        unet_hidden,
        control_hidden,
        steps,
        scale,
        control_time_first[0],
        control_time_second[0],
        control_proj[0].T,
        unet_time_first,
        unet_time_second,
        unet_proj.T,
        control_conv_first[0],
        control_conv_second[0],
        unet_conv_first,
        unet_conv_second,
        zero_conv[0],
    )


def solution(mesh):
    in_specs = (
        P(("branch", "dp"), "mp", None),
        P("branch", None, "dp", "mp", None),
        P(None, "dp"),
        P("branch", None, "dp"),
        P(),
        P(),
        P(None, "mp"),
        P(None, "mp", None),
        P(None, "mp", None),
        P("branch", None, None),
        P("branch", None, None),
        P("branch", None, "mp"),
        P("branch", None, "mp", None),
        P("branch", None, "mp", None),
        P("branch", "mp", None),
    )
    out_specs = P(("branch", "dp"), "mp", None)
    return jax.shard_map(shards, mesh=mesh, in_specs=in_specs, out_specs=out_specs, check_vma=False)
```

time: 74.8 us -> 67.1 us (0.90)
  Pallas kernels: 70.3 us -> 65.4 us
  other arithmetic: 1.47 us -> 0 us
  local copies, waits for them, and re-layouts: 2.87 us -> 1.59 us
    pallas_call x1, Pallas kernels: 70.3 us -> 65.4 us  [shards(): pl.pallas_call(functools.partial(kernel, ways), out_shape=jax.ShapeDtypeS...]
    squeeze x1 -> x0, local copies, waits for them, and re-layouts: 1.28 us -> none  [shards(): scale = control_scales[0]]
where the time goes in v1:
time: 67.1 us; the launch traced here: 67 us
  Pallas kernels  65.4 us (97%)
  local copies, waits for them, and re-layouts  1.59 us (2%)
    pallas_call x1, Pallas kernels, shards(): pl.pallas_call(functools.partial(kernel, ways), out_shape=jax.ShapeDtypeS...  65.4 us
    unnamed x1, local copies, waits for them, and re-layouts  1.59 us

profile of v1, /device:TPU:0, one launch (start us, length us, event | category | flops | bytes accessed | tf_op | source)
XLA Modules:
  0.0 67.0 jit_solution(11366883975788317746)
XLA Ops:
  0.0 65.4 %shard_map.145 = bf16[1,320,256]{2,1,0:T(8,128)(2,1)} custom-call(bf16[1,320,256]{2,1,0:T(8,128)(2,1)} %unet_hidden.1, bf16[1,2,1,320,256]{4,3,2,1,0:T(8,128)(2,1)} %control_hidden.1, s32[1,2]{1,0:T(1,128)} %bitcast.18, s32[1,2]{1,0:T(1,128)} %bitcast.19, bf16[320,1280]{1,0:T(8,128)(2,1)} %bitcast.14, bf16[1280,1280]{1,0:T(8,128)(2,1)} %bitcast.13, ...), custom_call_target="tpu_custom_call" | custom-call | tf_op jit(solution)/shard_map/pallas_call | solution.py:521
  65.4 1.6 %copy.17 = bf16[1,320,256]{2,1,0:T(8,128)(2,1)} copy(bf16[1,320,256]{2,1,0:T(8,128)(2,1)} %shard_map.145) | data formatting | bytes 327680

commit v2 on v1

v2 whole, which is shorter than its diff:
```python
import functools
import math

import jax
import jax.numpy as jnp
from jax import lax
from jax.experimental import pallas as pl
from jax.experimental.pallas import tpu as pltpu
from jax.sharding import PartitionSpec as P

TDIM = 320
GROUP = 40
PIECES = 2
PAIR_PIECES = 4
EDGE_FIRST = 2
SIDE = 16
MESH = pl.DeviceIdType.MESH


def sinusoid(steps, rows):
    half_width = TDIM // 2
    row = lax.broadcasted_iota(jnp.int32, (rows, TDIM), 0)
    spot = lax.broadcasted_iota(jnp.int32, (rows, TDIM), 1)
    place = jnp.where(spot < half_width, spot, spot - half_width).astype(jnp.float32)
    frequency = jnp.exp(-math.log(10000.0) * place / half_width)
    step = jnp.zeros((rows, TDIM), jnp.float32)
    for i, value in enumerate(steps):
        step = jnp.where(row == i, value.astype(jnp.float32), step)
    angles = step * frequency
    return jnp.where(spot < half_width, jnp.cos(angles), jnp.sin(angles))


def norm_silu(values):
    width, pixels = values.shape
    grouped = values.reshape(width // GROUP, GROUP, pixels)
    count = 1.0 / (GROUP * pixels)
    mean = jnp.sum(jnp.sum(grouped, axis=1, keepdims=True), axis=2, keepdims=True) * count
    centered = grouped - mean
    var = jnp.sum(jnp.sum(centered * centered, axis=1, keepdims=True), axis=2, keepdims=True) * count
    normed = centered * lax.rsqrt(var + 1e-05)
    return jax.nn.silu(normed).reshape(width, pixels)


def kernel(
    ways,
    unet_hidden,
    control_hidden,
    steps,
    scale,
    hbm_time_first_c,
    hbm_time_second_c,
    hbm_proj_c,
    hbm_time_first_u,
    hbm_time_second_u,
    hbm_proj_u,
    first_c,
    second_c,
    first_u,
    second_u,
    zero,
    out,
    time_first,
    time_second,
    proj,
    w1c,
    w2c,
    w1u,
    w2u,
    wz,
    gathered,
    above,
    below,
    taps,
    start,
    inner,
    sends,
    lands,
    far,
    pair_lands,
    pair_total,
    held,
    scaled,
    swap_out,
    swap_in,
    load_sem,
    ag_send,
    ag_recv,
    rs_send,
    rs_recv,
    far_recv,
    pair_send,
    pair_recv,
    z_send,
    z_recv,
    swap_send,
    swap_recv,
):
    branch = lax.axis_index("branch")
    dp = lax.axis_index("dp")
    me = lax.axis_index("mp")
    width, pixels = unet_hidden.shape[1], unet_hidden.shape[2]
    channels = ways * width
    last = ways - 1
    tile = 256
    chunks = channels // tile
    scope = jax.named_scope

    loads = [
        pltpu.make_async_copy(src, dst, load_sem.at[i])
        for i, (src, dst) in enumerate(
            (
                (hbm_time_first_c, time_first.at[0]),
                (hbm_time_second_c, time_second.at[0]),
                (hbm_proj_c, proj.at[0]),
                (hbm_time_first_u, time_first.at[1]),
                (hbm_time_second_u, time_second.at[1]),
                (hbm_proj_u, proj.at[1]),
                (first_c, w1c),
                (second_c, w2c),
                (first_u, w1u),
                (second_u, w2u),
                (zero, wz.at[pl.ds(pl.multiple_of(lax.rem(me, 2) * width, width), width)]),
            )
        )
    ]
    for i in (0, 1, 2, 6):
        loads[i].start()

    barrier = pltpu.get_barrier_semaphore()

    def greet(inside, coord):
        @pl.when(inside)
        def _():
            pl.semaphore_signal(barrier, inc=1, device_id=coord, device_id_type=MESH)

    greet(me < last, (branch, dp, me + 1))
    greet(me > 0, (branch, dp, me - 1))
    pl.semaphore_signal(barrier, inc=1, device_id=(1 - branch, dp, me), device_id_type=MESH)

    planes = lax.axis_size("dp")
    for place in range(planes):

        @pl.when(dp != place)
        def _():
            pl.semaphore_signal(barrier, inc=1, device_id=(branch, place, me), device_id_type=MESH)

    def wait_barrier():
        rim = (me == 0) | (me == last)

        @pl.when(rim)
        def _():
            pl.semaphore_wait(barrier, 1 + planes)

        @pl.when(jnp.logical_not(rim))
        def _():
            pl.semaphore_wait(barrier, 2 + planes)

    def rows_of(slot, piece=None):
        if piece is None:
            return pl.ds(pl.multiple_of(slot * width, width), width)
        size = width // PIECES
        return pl.ds(pl.multiple_of(slot * width + piece * size, size), size)

    def strip(piece):
        return pl.ds(piece * (width // PIECES), width // PIECES)

    middle = ways // 2
    low, high = me < middle, me >= middle

    def ag_copy(unit, side, hop, slot, piece):
        return pltpu.make_async_remote_copy(
            src_ref=gathered.at[unit, rows_of(slot, piece)],
            dst_ref=gathered.at[unit, rows_of(slot, piece)],
            send_sem=ag_send.at[unit, side, hop, piece],
            recv_sem=ag_recv.at[unit, side, hop, piece],
            device_id=(branch, dp, me + 1 - 2 * side),
            device_id_type=MESH,
        )


    def forward(unit, hop, sides):
        for piece in range(PIECES):
            for side, half in ((0, low), (1, high), (0, high), (1, low)):
                if half is (high if side == 0 else low) and sides is inward:
                    continue
                if half is (low if side == 0 else high) and sides is outward:
                    continue
                from_slot = me - hop if side == 0 else me + hop
                here = (from_slot >= 0) & (from_slot <= last)
                onward = here & ((me < last) if side == 0 else (me > 0)) & half & sides[side]

                @pl.when(onward)
                def _():
                    if hop > 0:
                        ag_copy(unit, side, hop - 1, from_slot, piece).wait_recv()
                    ag_copy(unit, side, hop, from_slot, piece).start()

    low, high = me < middle, me >= middle

    def ag_copy(unit, side, hop, slot, piece):
        return pltpu.make_async_remote_copy(
            src_ref=gathered.at[unit, rows_of(slot, piece)],
            dst_ref=gathered.at[unit, rows_of(slot, piece)],
            send_sem=ag_send.at[unit, side, hop, piece],
            recv_sem=ag_recv.at[unit, side, hop, piece],
            device_id=(branch, dp, me + 1 - 2 * side),
            device_id_type=MESH,
        )


    def forward(unit, hop, sides):
        for piece in range(PIECES):
            for side in range(2):
                from_slot = me - hop if side == 0 else me + hop
                here = (from_slot >= 0) & (from_slot <= last)
                onward = here & ((me < last) if side == 0 else (me > 0)) & sides[side]

                @pl.when(onward)
                def _():
                    if hop > 0:
                        ag_copy(unit, side, hop - 1, from_slot, piece).wait_recv()
                    ag_copy(unit, side, hop, from_slot, piece).start()

    edge = (me == 0) | (me == last)
    centre = jnp.logical_not(edge)
    inner_low, inner_high = low & jnp.logical_not(edge), high & jnp.logical_not(edge)
    both, inward, outward = (True, True), (low, high), (high, low)

    def ag_begin(unit, sides=both):
        forward(unit, 0, sides)

    def ag_inward(unit):
        for hop in range(1, last):
            forward(unit, hop, inward)

    def ag_outward(unit, hop):
        forward(unit, hop, outward)

    def ag_arrive(unit, passed):
        for hop in passed:
            for side in range(2):
                from_slot = me - hop if side == 0 else me + hop
                here = (from_slot >= 0) & (from_slot <= last)
                if hop < last:
                    here = here & ((me == last) if side == 0 else (me == 0))

                @pl.when(here)
                def _():
                    for piece in range(PIECES):
                        ag_copy(unit, side, hop - 1, from_slot, piece).wait_recv()

    def ag_drain(unit):
        for hop in range(last):
            for side in range(2):
                from_slot = me - hop if side == 0 else me + hop
                here = (from_slot >= 0) & (from_slot <= last)
                onward = here & ((me < last) if side == 0 else (me > 0))

                @pl.when(onward)
                def _():
                    for piece in range(PIECES):
                        ag_copy(unit, side, hop, from_slot, piece).wait_send()

    def rs_copy(side, dest, piece):
        return pltpu.make_async_remote_copy(
            src_ref=sends.at[2, rows_of(dest, piece)],
            dst_ref=lands.at[side, dest, strip(piece)],
            send_sem=rs_send.at[dest, piece],
            recv_sem=rs_recv.at[side, dest, piece],
            device_id=(branch, dp, me + 1 - 2 * side),
            device_id_type=MESH,
        )

    def far_copy(dest, piece):
        return pltpu.make_async_remote_copy(
            src_ref=sends.at[2, rows_of(dest, piece)],
            dst_ref=far.at[strip(piece)],
            send_sem=rs_send.at[dest, piece],
            recv_sem=far_recv.at[piece],
            device_id=(branch, dp, dest),
            device_id_type=MESH,
        )

    def fold_begin(group):
        ready = EDGE_FIRST * tile // width
        for rank in range(ready) if group == 0 else range(ready, last):
            for side, end in ((0, 0), (1, last)):
                dest = last - rank if side == 0 else rank

                @pl.when(me == end)
                def _():
                    for piece in range(PIECES):
                        rs_copy(side, dest, piece).start()

        if group == 0:
            return
        for side in range(2):
            rim = middle - side
            for dest in range(rim + 1, ways) if side == 0 else range(rim):

                @pl.when((me == rim) & centre)
                def _():
                    for piece in range(PIECES):
                        rs_copy(side, dest, piece).start()

    def fold_slots():
        for rank, piece, side in [
            (r, p, d) for r in range(last - 1) for p in range(PIECES) for d in range(2)
        ]:
            dest = last - rank if side == 0 else rank
            place = me if side == 0 else last - me
            rim = (place == middle - 1) & (rank < middle)
            onward = (place >= 1) & (place != middle) & (place < last - rank)

            @pl.when(onward)
            def _():
                rs_copy(side, dest, piece).wait_recv()
                added = sends[2, rows_of(dest, piece), :].astype(jnp.float32) + lands[
                    side, dest, strip(piece), :
                ].astype(jnp.float32)
                sends[2, rows_of(dest, piece), :] = added.astype(jnp.bfloat16)

            @pl.when(onward & rim)
            def _():
                far_copy(dest, piece).start()

            @pl.when(onward & jnp.logical_not(rim))
            def _():
                rs_copy(side, dest, piece).start()

    def fold_drain():
        for dest in range(ways):

            @pl.when(me != dest)
            def _():
                for piece in range(PIECES):
                    rs_copy(0, dest, piece).wait_send()

    double = 2 * width
    pairs = ways // 2
    mine = me // 2
    parity = lax.rem(me, 2)
    inwards = jnp.where(low, me + 1, me - 1)
    side_near = jnp.where(low, 0, 1)
    side_far = jnp.where(low, 1, 0)
    part = double // PAIR_PIECES

    def pair_copy(unit, side, pair, piece):
        return pltpu.make_async_remote_copy(
            src_ref=sends.at[unit, pl.ds(pair * double + piece * part, part)],
            dst_ref=pair_lands.at[unit, side, pair, pl.ds(piece * part, part)],
            send_sem=pair_send.at[unit, pair, piece],
            recv_sem=pair_recv.at[unit, side, pair, piece],
            device_id=(branch, dp, me + 1 - 2 * side),
            device_id_type=MESH,
        )

    def pair_order(side):
        return range(pairs - 1, -1, -1) if side == 0 else range(pairs)

    def pair_begin(unit):
        for side, end in ((0, 0), (1, last)):

            @pl.when(me == end)
            def _():
                for pair in pair_order(side):
                    if pair != end // 2:
                        for piece in range(PAIR_PIECES):
                            pair_copy(unit, side, pair, piece).start()

    def pair_slot(unit):
        for side in range(2):
            for pair in pair_order(side):
                beyond = (pair > mine) if side == 0 else (pair < mine)

                @pl.when(centre & beyond)
                def _():
                    for piece in range(PAIR_PIECES):
                        pair_copy(unit, side, pair, piece).wait_recv()
                        rows = pl.ds(pair * double + piece * part, part)
                        added = sends[unit, rows, :].astype(jnp.float32) + pair_lands[
                            unit, side, pair, pl.ds(piece * part, part), :
                        ].astype(jnp.float32)
                        sends[unit, rows, :] = added.astype(jnp.bfloat16)
                        pair_copy(unit, side, pair, piece).start()

    def pair_drain(unit):
        for pair in range(pairs):
            for side, beyond in ((0, pair > mine), (1, pair < mine)):

                @pl.when(beyond)
                def _():
                    for piece in range(PAIR_PIECES):
                        pair_copy(unit, side, pair, piece).wait_send()

    shares = math.gcd(width // 8, planes)
    share = width // shares
    sharing = dp < shares
    mate = me + 1 - 2 * parity

    def share_rows(holder, place):
        row = lax.rem(holder, 2) * width + place * share
        return pl.ds(pl.multiple_of(row, share), share)

    def cross_copy():
        return pltpu.make_async_remote_copy(
            src_ref=zero.at[pl.ds(pl.multiple_of(dp * share, share), share)],
            dst_ref=wz.at[share_rows(me, dp)],
            send_sem=z_send.at[dp],
            recv_sem=z_recv.at[dp],
            device_id=(branch, dp, mate),
            device_id_type=MESH,
        )

    def cross_begin(chosen):
        @pl.when(chosen & sharing)
        def _():
            cross_copy().start()

    def plane_copy(source, target):
        return pltpu.make_async_remote_copy(
            src_ref=wz.at[share_rows(mate, source)],
            dst_ref=wz.at[share_rows(mate, source)],
            send_sem=z_send.at[target],
            recv_sem=z_recv.at[source],
            device_id=(branch, target, me),
            device_id_type=MESH,
        )

    def plane_begin():
        @pl.when(sharing)
        def _():
            cross_copy().wait_recv()

        for place in range(planes):

            @pl.when(sharing & (dp != place))
            def _():
                plane_copy(dp, place).start()

    def plane_arrive():
        loads[10].wait()
        for place in range(shares):

            @pl.when(dp != place)
            def _():
                plane_copy(place, place).wait_recv()

    def plane_drain():
        @pl.when(sharing)
        def _():
            cross_copy().wait_send()

        for place in range(planes):

            @pl.when(sharing & (dp != place))
            def _():
                plane_copy(dp, place).wait_send()

    def own_hidden(unit):
        if unit == 2:
            return unet_hidden[0]
        image = 1 - branch if unit == 0 else branch
        return control_hidden[0, image, 0]

    def prepare(unit):
        gathered[unit, rows_of(me), :] = norm_silu(own_hidden(unit).astype(jnp.float32)).astype(
            jnp.bfloat16
        )

    def embed(block, waves):
        for load in loads[3 * block : 3 * block + 3]:
            load.wait()
        act = waves
        for weight in (time_first, time_second):
            act = jax.nn.silu(
                jnp.dot(act, weight[block], preferred_element_type=jnp.float32)
            ).astype(jnp.bfloat16)
        start[block] = lax.dot_general(
            proj[block], act, (((1,), (1,)), ((), ())), preferred_element_type=jnp.float32
        )

    def column_kept(shape, axis, dx):
        spot = lax.rem(lax.broadcasted_iota(jnp.int32, shape, axis), SIDE) + dx
        return (spot >= 0) & (spot < SIDE)

    def shift_rows(unit, rows):
        spot = lax.broadcasted_iota(jnp.int32, (1, pixels), 1)
        whole = gathered[unit, rows, :].astype(jnp.float32)
        down = pltpu.roll(whole, SIDE, 1)
        above[rows, :] = jnp.where(spot >= SIDE, down, 0.0).astype(jnp.bfloat16)
        up = pltpu.roll(whole, pixels - SIDE, 1)
        below[rows, :] = jnp.where(spot < pixels - SIDE, up, 0.0).astype(jnp.bfloat16)

    def first_conv(unit, weight, half=None):
        if half is None:
            rows = slice(0, channels)
        else:
            rows = pl.ds(pl.multiple_of(half * (channels // 2), channels // 2), channels // 2)
        shift_rows(unit, rows)

        def side_term(dx):
            term = None
            sources = (above[rows, :], gathered[unit, rows, :], below[rows, :])
            for line, source in enumerate(sources):
                product = jnp.dot(
                    weight[3 * line + dx + 1, :, rows],
                    source,
                    preferred_element_type=jnp.float32,
                )
                term = product if term is None else term + product
            return term

        if half is side_far:
            inner[...] += side_term(0)
        else:
            other = branch == 1 if unit == 0 else branch == 0
            columns = start[unit // 2]
            inner[...] = side_term(0) + jnp.where(other, columns[:, :1], columns[:, 1:2])
        for dx in (-1, 1):
            moved = pltpu.roll(side_term(dx), (pixels - dx) % pixels, 1)
            inner[...] += jnp.where(column_kept((1, pixels), 1, dx), moved, 0.0)

    def fill_taps():
        flipped = norm_silu(inner[...]).T
        operands = []
        for dx in (-1, 0, 1):
            moved = flipped if dx == 0 else pltpu.roll(flipped, (pixels - dx) % pixels, 0)
            operands.append(jnp.where(column_kept((pixels, 1), 0, dx), moved, 0.0))
        taps[SIDE : SIDE + pixels, :] = jnp.concatenate(operands, axis=1).astype(jnp.bfloat16)


    def columns_of(chunk):
        return slice(chunk * tile, (chunk + 1) * tile)

    def second_chunk(weight, chunk):
        total = None
        for line in range(3):
            product = jnp.dot(
                taps[SIDE * line : SIDE * line + pixels, :],
                weight[3 * line : 3 * line + 3, :, columns_of(chunk)].reshape(3 * width, tile),
                preferred_element_type=jnp.float32,
            )
            total = product if total is None else total + product
        return total

    def residual_chunk(chunk):
        at = columns_of(chunk)
        term = jnp.dot(scaled[...], wz[:, at], preferred_element_type=jnp.float32)
        return term + swap_in[:, at].astype(jnp.float32)

    def second_conv(unit, weight):
        for chunk in range(chunks):
            total = second_chunk(weight, chunk)
            sends[unit, columns_of(chunk), :] = total.T.astype(jnp.bfloat16)
        pair_begin(unit)

    def edge_conv(order, first):
        for chunk in order[:first]:
            total = second_chunk(w2u, chunk) + residual_chunk(chunk)
            sends[2, columns_of(chunk), :] = total.T.astype(jnp.bfloat16)

    def edge_last():
        for half, order in ((low, range(chunks - 1, -1, -1)), (high, range(chunks))):

            @pl.when(half)
            def _():
                edge_conv(order, EDGE_FIRST)
                if EDGE_FIRST < chunks:
                    fold_begin(0)
                    edge_conv(order[EDGE_FIRST:], chunks)

        if EDGE_FIRST == chunks:
            fold_begin(0)
        fold_begin(1)

    def centre_conv():
        for chunk in range(chunks):
            held[columns_of(chunk), :] = second_chunk(w2u, chunk).T

    def centre_last():
        for chunk in range(chunks):
            at = columns_of(chunk)
            sends[2, at, :] = (held[at, :] + residual_chunk(chunk).T).astype(jnp.bfloat16)
        fold_begin(1)

    def collect():
        inner[...] = own_hidden(2).astype(jnp.float32) + sends[2, rows_of(me), :].astype(
            jnp.float32
        )
        left, right = (me > 0) & (me != middle), (me < last) & (me != middle - 1)
        for side, inside in ((0, left), (1, right)):

            @pl.when(inside)
            def _():
                for piece in range(PIECES):
                    rs_copy(side, me, piece).wait_recv()
                inner[...] += lands[side, me].astype(jnp.float32)

        for piece in range(PIECES):
            far_copy(inwards, piece).wait_recv()
        return inner[...] + far[...].astype(jnp.float32)

    def scale_copy(unit):
        image = 1 - branch if unit == 0 else branch
        factor = scale[0, image].astype(jnp.float32) * 0.125
        pair_total[...] = sends[
            unit, pl.ds(pl.multiple_of(mine * double, double), double), :
        ].astype(jnp.float32)
        own = pl.ds(pl.multiple_of(parity * width, width), width)
        pair_total[own, :] += own_hidden(unit).astype(jnp.float32)
        for pair in range(pairs):
            for side in range(2):

                @pl.when(centre & (mine == pair) & (parity == side))
                def _():
                    for piece in range(PAIR_PIECES):
                        pair_copy(unit, side, pair, piece).wait_recv()
                    pair_total[...] += pair_lands[unit, side, pair].astype(jnp.float32)

        scaled[...] = (pair_total[...] * factor).T.astype(jnp.bfloat16)

    swap = pltpu.make_async_remote_copy(
        src_ref=swap_out,
        dst_ref=swap_in,
        send_sem=swap_send,
        recv_sem=swap_recv,
        device_id=(1 - branch, dp, me),
        device_id_type=MESH,
    )

    def first_residual():
        scale_copy(0)
        swap_out[...] = jnp.dot(scaled[...], wz[...], preferred_element_type=jnp.float32).astype(
            jnp.bfloat16
        )
        swap.start()

    taps[0:SIDE, :] = jnp.zeros((SIDE, 3 * width), jnp.bfloat16)
    taps[SIDE + pixels :, :] = jnp.zeros((SIDE, 3 * width), jnp.bfloat16)

    hops = range(1, last)
    with scope("prep"):
        for unit in range(3):
            prepare(unit)
        waves = sinusoid([steps[0, i] for i in range(steps.shape[1])], 16).astype(jnp.bfloat16)
    with scope("barrier"):
        wait_barrier()
    with scope("ag0"):
        ag_begin(0)
        cross_begin(centre)
        for unit in (1, 2):
            ag_begin(unit, (me == 0, me == last))
        cross_begin(edge)
    with scope("embed0"):
        embed(0, waves)
        for i in (7, 3, 4, 5, 10):
            loads[i].start()
    for hop in hops:
        with scope(f"ag0_hop{hop}"):
            forward(0, hop, both)
            if hop == 1:
                ag_begin(1, (inner_low, inner_high))
    with scope("ag1"):
        ag_begin(1, outward)
        ag_inward(1)
    with scope("embed1"):
        embed(1, waves)
    with scope("ag0_wait"):
        ag_arrive(0, range(1, ways))
    with scope("w1c_wait"):
        loads[6].wait()
    with scope("conv1_0"):
        first_conv(0, w1c)
    with scope("ag2_in"):
        ag_begin(2, (inner_low, inner_high))
        ag_inward(2)
    with scope("ag1_out1"):
        ag_outward(1, 1)
        for i in (8, 9):
            loads[i].start()
    with scope("w2c_wait"):
        loads[7].wait()
    with scope("fill0"):
        fill_taps()
    with scope("conv2_0"):
        second_conv(0, w2c)
    for hop in hops[1:]:
        with scope(f"ag1_out{hop}"):
            ag_outward(1, hop)
    with scope("ag2"):
        ag_begin(2, outward)
    with scope("plane"):
        plane_begin()
    with scope("ag1_wait"):
        ag_arrive(1, range(1, ways))
    with scope("conv1_1"):
        first_conv(1, w1c)
    with scope("ag2_out1"):
        ag_outward(2, 1)
    with scope("fill1"):
        fill_taps()
    for hop in hops[1:]:
        with scope(f"ag2_out{hop}"):
            ag_outward(2, hop)
    with scope("conv2_1"):
        second_conv(1, w2c)
    with scope("rs0_slot"):
        pair_slot(0)
    with scope("plane_wait"):
        plane_arrive()
    with scope("res0e"):
        pl.when(edge)(first_residual)
    with scope("ag2_wait"):
        ag_arrive(2, range(1, middle))
        loads[8].wait()
    with scope("conv1_2n"):
        first_conv(2, w1u, side_near)
    with scope("ag2_wait2"):
        ag_arrive(2, range(middle, ways))
        loads[9].wait()
    with scope("conv1_2f"):
        first_conv(2, w1u, side_far)
    with scope("res0c"):
        pl.when(centre)(first_residual)
    with scope("fill2"):
        fill_taps()

    @pl.when(edge)
    def _():
        with scope("res1e"):
            scale_copy(1)
        with scope("swap_e"):
            swap.wait_recv()
        with scope("conv2_2e"):
            edge_last()

    @pl.when(centre)
    def _():
        with scope("conv2_2c"):
            centre_conv()
        with scope("rs1_slot"):
            pair_slot(1)
        with scope("res1c"):
            scale_copy(1)
        with scope("swap_c"):
            swap.wait_recv()
        with scope("add_c"):
            centre_last()

    with scope("rs2_slots"):
        fold_slots()
    with scope("collect2"):
        out[0] = collect().astype(jnp.bfloat16)
    with scope("drain"):
        swap.wait_send()
        plane_drain()
        for unit in range(3):
            ag_drain(unit)
        for unit in range(2):
            pair_drain(unit)
        fold_drain()


def shards(
    unet_hidden,
    control_hidden,
    timesteps,
    control_scales,
    unet_time_first,
    unet_time_second,
    unet_proj,
    unet_conv_first,
    unet_conv_second,
    control_time_first,
    control_time_second,
    control_proj,
    control_conv_first,
    control_conv_second,
    zero_conv,
):
    ways, planes = lax.axis_size("mp"), lax.axis_size("dp")
    width, pixels = unet_hidden.shape[1], unet_hidden.shape[2]
    channels = ways * width
    halves = timesteps.shape[0]
    steps = timesteps.reshape(1, halves)
    scale = control_scales.reshape(1, halves)
    vmem = pl.BlockSpec(memory_space=pltpu.VMEM)
    smem = pl.BlockSpec(memory_space=pltpu.SMEM)
    hbm = pl.BlockSpec(memory_space=pl.ANY)
    taps = unet_conv_first.shape[0]
    bf16, f32 = jnp.bfloat16, jnp.float32
    conv_shape = (taps, width, channels)
    return pl.pallas_call(
        functools.partial(kernel, ways),
        out_shape=pltpu.VMEM((1, width, pixels), bf16),
        in_specs=[vmem] * 2 + [smem] * 2 + [hbm] * 11,
        out_specs=vmem,
        scratch_shapes=[
            pltpu.VMEM((2,) + unet_time_first.shape, bf16),
            pltpu.VMEM((2,) + unet_time_second.shape, bf16),
            pltpu.VMEM((2,) + unet_proj.shape[::-1], bf16),
            pltpu.VMEM(conv_shape, bf16),
            pltpu.VMEM(conv_shape, bf16),
            pltpu.VMEM(conv_shape, bf16),
            pltpu.VMEM(conv_shape, bf16),
            pltpu.VMEM((2 * width, channels), bf16),
            pltpu.VMEM((3, channels, pixels), bf16),
            pltpu.VMEM((channels, pixels), bf16),
            pltpu.VMEM((channels, pixels), bf16),
            pltpu.VMEM((pixels + 2 * SIDE, 3 * width), bf16),
            pltpu.VMEM((2, width, 16), f32),
            pltpu.VMEM((width, pixels), f32),
            pltpu.VMEM((3, channels, pixels), bf16),
            pltpu.VMEM((2, ways, width, pixels), bf16),
            pltpu.VMEM((width, pixels), bf16),
            pltpu.VMEM((2, 2, ways // 2, 2 * width, pixels), bf16),
            pltpu.VMEM((2 * width, pixels), f32),
            pltpu.VMEM((channels, pixels), f32),
            pltpu.VMEM((pixels, 2 * width), bf16),
            pltpu.VMEM((pixels, channels), bf16),
            pltpu.VMEM((pixels, channels), bf16),
            pltpu.SemaphoreType.DMA((11,)),
            pltpu.SemaphoreType.DMA((3, 2, ways - 1, PIECES)),
            pltpu.SemaphoreType.DMA((3, 2, ways - 1, PIECES)),
            pltpu.SemaphoreType.DMA((ways, PIECES)),
            pltpu.SemaphoreType.DMA((2, ways, PIECES)),
            pltpu.SemaphoreType.DMA((PIECES,)),
            pltpu.SemaphoreType.DMA((2, ways // 2, PAIR_PIECES)),
            pltpu.SemaphoreType.DMA((2, 2, ways // 2, PAIR_PIECES)),
            pltpu.SemaphoreType.DMA((planes,)),
            pltpu.SemaphoreType.DMA((planes,)),
            pltpu.SemaphoreType.DMA,
            pltpu.SemaphoreType.DMA,
        ],
        compiler_params=pltpu.CompilerParams(
            collective_id=0, has_side_effects=True, vmem_limit_bytes=60 * 1024 * 1024
        ),
    )(
        unet_hidden,
        control_hidden,
        steps,
        scale,
        control_time_first[0],
        control_time_second[0],
        control_proj[0].T,
        unet_time_first,
        unet_time_second,
        unet_proj.T,
        control_conv_first[0],
        control_conv_second[0],
        unet_conv_first,
        unet_conv_second,
        zero_conv[0],
    )


def solution(mesh):
    in_specs = (
        P(("branch", "dp"), "mp", None),
        P("branch", None, "dp", "mp", None),
        P(None, "dp"),
        P("branch", None, "dp"),
        P(),
        P(),
        P(None, "mp"),
        P(None, "mp", None),
        P(None, "mp", None),
        P("branch", None, None),
        P("branch", None, None),
        P("branch", None, "mp"),
        P("branch", None, "mp", None),
        P("branch", None, "mp", None),
        P("branch", "mp", None),
    )
    out_specs = P(("branch", "dp"), "mp", None)
    return jax.shard_map(shards, mesh=mesh, in_specs=in_specs, out_specs=out_specs, check_vma=False)
```

time: 67.1 us -> 60.8 us (0.906)
  Pallas kernels: 65.4 us -> 59.6 us
  local copies, waits for them, and re-layouts: 1.59 us -> 0.67 us
    pallas_call x1, Pallas kernels: 65.4 us -> 59.6 us  [shards(): pl.pallas_call(functools.partial(kernel, ways), out_shape=pltpu.VMEM((1,...]
    unnamed x1, local copies, waits for them, and re-layouts: 1.59 us -> 0.67 us
where the time goes in v2:
time: 60.8 us; the launch traced here: 60.3 us
  Pallas kernels  59.6 us (98%)
  local copies, waits for them, and re-layouts  0.67 us (1%)
    pallas_call x1, Pallas kernels, shards(): pl.pallas_call(functools.partial(kernel, ways), out_shape=pltpu.VMEM((1,...  59.6 us

profile of v2, /device:TPU:0, one launch (start us, length us, event | category | flops | bytes accessed | tf_op | source)
XLA Modules:
  0.0 60.3 jit_solution(14944142367735578125)
XLA Ops:
  0.0 59.6 %shard_map.145 = bf16[1,320,256]{2,1,0:T(8,128)(2,1)S(1)} custom-call(bf16[1,320,256]{2,1,0:T(8,128)(2,1)} %unet_hidden.1, bf16[1,2,1,320,256]{4,3,2,1,0:T(8,128)(2,1)} %control_hidden.1, s32[1,2]{1,0:T(1,128)} %bitcast.18, s32[1,2]{1,0:T(1,128)} %bitcast.19, bf16[320,1280]{1,0:T(8,128)(2,1)} %bitcast.14, bf16[1280,1280]{1,0:T(8,128)(2,1)} %bitcast.13, ...), custom_call_target="tpu_custom_call" | custom-call | tf_op jit(solution)/shard_map/pallas_call | solution.py:794
  59.6 0.7 %copy.17 = bf16[1,320,256]{2,1,0:T(8,128)(2,1)} copy(bf16[1,320,256]{2,1,0:T(8,128)(2,1)S(1)} %shard_map.145) | data formatting | bytes 327680

commit v3 on v2

--- a/solution.py
+++ b/solution.py
@@ -225,6 +225,8 @@
     centre = jnp.logical_not(edge)
     inner_low, inner_high = low & jnp.logical_not(edge), high & jnp.logical_not(edge)
     both, inward, outward = (True, True), (low, high), (high, low)
+    early, late = branch == 1, branch == 0
+    outward_early, outward_late = (high & early, low & early), (high & late, low & late)
 
     def ag_begin(unit, sides=both):
         forward(unit, 0, sides)
@@ -545,9 +547,18 @@
         return total
 
     def residual_chunk(chunk):
-        at = columns_of(chunk)
-        term = jnp.dot(scaled[...], wz[:, at], preferred_element_type=jnp.float32)
-        return term + swap_in[:, at].astype(jnp.float32)
+        return jnp.dot(
+            scaled[...], wz[:, columns_of(chunk)], preferred_element_type=jnp.float32
+        )
+
+    def swapped(chunk):
+        return swap_in[:, columns_of(chunk)].astype(jnp.float32)
+
+    def edge_residual():
+        first_residual()
+        scale_copy(1)
+        for chunk in range(chunks):
+            held[columns_of(chunk), :] = residual_chunk(chunk).T
 
     def second_conv(unit, weight):
         for chunk in range(chunks):
@@ -557,8 +568,9 @@
 
     def edge_conv(order, first):
         for chunk in order[:first]:
-            total = second_chunk(w2u, chunk) + residual_chunk(chunk)
-            sends[2, columns_of(chunk), :] = total.T.astype(jnp.bfloat16)
+            at = columns_of(chunk)
+            total = second_chunk(w2u, chunk) + swapped(chunk)
+            sends[2, at, :] = (held[at, :] + total.T).astype(jnp.bfloat16)
 
     def edge_last():
         for half, order in ((low, range(chunks - 1, -1, -1)), (high, range(chunks))):
@@ -581,7 +593,8 @@
     def centre_last():
         for chunk in range(chunks):
             at = columns_of(chunk)
-            sends[2, at, :] = (held[at, :] + residual_chunk(chunk).T).astype(jnp.bfloat16)
+            total = residual_chunk(chunk) + swapped(chunk)
+            sends[2, at, :] = (held[at, :] + total.T).astype(jnp.bfloat16)
         fold_begin(1)
 
     def collect():
@@ -689,7 +702,7 @@
         with scope(f"ag1_out{hop}"):
             ag_outward(1, hop)
     with scope("ag2"):
-        ag_begin(2, outward)
+        ag_begin(2, outward_early)
     with scope("plane"):
         plane_begin()
     with scope("ag1_wait"):
@@ -697,20 +710,24 @@
     with scope("conv1_1"):
         first_conv(1, w1c)
     with scope("ag2_out1"):
-        ag_outward(2, 1)
+        forward(2, 1, outward_early)
     with scope("fill1"):
         fill_taps()
     for hop in hops[1:]:
         with scope(f"ag2_out{hop}"):
-            ag_outward(2, hop)
+            forward(2, hop, outward_early)
     with scope("conv2_1"):
         second_conv(1, w2c)
     with scope("rs0_slot"):
         pair_slot(0)
+    with scope("ag2_late"):
+        ag_begin(2, outward_late)
+        for hop in hops:
+            forward(2, hop, outward_late)
     with scope("plane_wait"):
         plane_arrive()
     with scope("res0e"):
-        pl.when(edge)(first_residual)
+        pl.when(edge)(edge_residual)
     with scope("ag2_wait"):
         ag_arrive(2, range(1, middle))
         loads[8].wait()
@@ -728,8 +745,6 @@
 
     @pl.when(edge)
     def _():
-        with scope("res1e"):
-            scale_copy(1)
         with scope("swap_e"):
             swap.wait_recv()
         with scope("conv2_2e"):

time: 60.8 us -> 60.4 us (level)
  no operation moved by 1% of the time
where the time goes in v3:
time: 60.4 us; the launch traced here: 60.2 us
  Pallas kernels  59.6 us (99%)
  local copies, waits for them, and re-layouts  0.67 us (1%)
    pallas_call x1, Pallas kernels, shards(): pl.pallas_call(functools.partial(kernel, ways), out_shape=pltpu.VMEM((1,...  59.6 us

profile of v3, /device:TPU:0, one launch (start us, length us, event | category | flops | bytes accessed | tf_op | source)
XLA Modules:
  0.0 60.2 jit_solution(1267170520471252780)
XLA Ops:
  0.0 59.6 %shard_map.145 = bf16[1,320,256]{2,1,0:T(8,128)(2,1)S(1)} custom-call(bf16[1,320,256]{2,1,0:T(8,128)(2,1)} %unet_hidden.1, bf16[1,2,1,320,256]{4,3,2,1,0:T(8,128)(2,1)} %control_hidden.1, s32[1,2]{1,0:T(1,128)} %bitcast.18, s32[1,2]{1,0:T(1,128)} %bitcast.19, bf16[320,1280]{1,0:T(8,128)(2,1)} %bitcast.14, bf16[1280,1280]{1,0:T(8,128)(2,1)} %bitcast.13, ...), custom_call_target="tpu_custom_call" | custom-call | tf_op jit(solution)/shard_map/pallas_call | solution.py:809
  59.6 0.7 %copy.17 = bf16[1,320,256]{2,1,0:T(8,128)(2,1)} copy(bf16[1,320,256]{2,1,0:T(8,128)(2,1)S(1)} %shard_map.145) | data formatting | bytes 327680
